TPU v7x, 32 devices: a whole 2x2x4 slice. The times are simulated.
32 devices in a mesh: gx: 4 (over x, core), gy: 4 (over z), gz: 2 (over y).
Axes of the slice: x: 2, y: 2, z: 4, core: 2. Of those that a mesh axis runs over, the one named last changes fastest.
Arguments:
- layer_input: bfloat16 [1024, 4096], P('gz', ('gx', 'gy')), may hold values from -6 to 6
- modality: int32 [1024], P('gz'), may hold values 0 or 1
- image_spans: int32 [2, 8], replicated, may hold values from 0 to 1024, as said below
- norm_gain: float32 [2, 4096], P(None, ('gx', 'gy')), may hold values from 0.1 to 1.9
- w_qkv: bfloat16 [3, 4096, 2048], P(None, 'gz', ('gx', 'gy')), as said below
- w_out: bfloat16 [2048, 4096], P(('gx', 'gy'), 'gz'), may hold values from -0.125 to 0.125
- grad_out: bfloat16 [1024, 4096], P('gz', ('gx', 'gy')), may hold values from -6 to 6
Outputs:
- attn_out: bfloat16 [1024, 4096], P('gz', ('gx', 'gy'))
- grad_in: bfloat16 [1024, 4096], P('gz', ('gx', 'gy'))
- grad_qkv: float32 [3, 4096, 2048], P(None, 'gz', ('gx', 'gy'))
- grad_wout: float32 [2048, 4096], P(('gx', 'gy'), 'gz')
- grad_gain: float32 [2, 4096], P(None, ('gx', 'gy'))
Inputs may be any that keep to these rules, and one draw needn't show every extreme that they name: `image_spans`: row 0 holds the first position of each of 8 image spans, in increasing order, and row 1 one past its last; spans are disjoint and none is empty. `w_qkv`: entries are at most 20 * 4096 ** -0.5 in magnitude.
All inputs are finite; a program needn't handle non-finite values. No bound on the sum of `modality` on one device may be relied on, other than what follows from the above.
Results may differ from a plain program's by a relative error of at most 0.035.
The roundings to bfloat16 on the way count: a program that leaves them out, or rounds other values in their place, can miss the bound.
Values may be sent and summed in bfloat16 or wider, within the bound.
A program may use at most 128 MiB of HBM per device.

v0:
```python
import math
import jax
import jax.numpy as jnp
from jax import lax
from jax.sharding import PartitionSpec as P

epsilon = 1e-05
masked_low = -1e30


def span_index(positions, image_spans):
    inside = (positions[:, None] >= image_spans[0][None, :]) & (
        positions[:, None] < image_spans[1][None, :]
    )
    labels = jnp.arange(1, image_spans.shape[1] + 1, dtype=jnp.int32)
    return jnp.sum(jnp.where(inside, labels[None, :], 0), axis=1) - 1


def visible(query_pos, query_span, key_pos, key_span):
    causal = key_pos[None, :] <= query_pos[:, None]
    same_image = (query_span[:, None] == key_span[None, :]) & (query_span[:, None] >= 0)
    return causal | same_image


def per_device(layer_input, modality, image_spans, norm_gain, w_qkv, w_out, grad_out):
    tok_rows, local_width = layer_input.shape
    full_width = local_width * lax.axis_size(("gx", "gy"))
    head_dim = w_qkv.shape[2]
    inputs_f = layer_input.astype(jnp.float32)
    squares = lax.psum(jnp.sum(inputs_f * inputs_f, axis=1), ("gx", "gy"))
    inv_rms = lax.rsqrt(squares / full_width + epsilon)
    row_gain = jnp.where(modality[:, None] == 1, norm_gain[1][None, :], norm_gain[0][None, :])
    scaled = inputs_f * inv_rms[:, None]
    normed = (scaled * row_gain).astype(jnp.bfloat16)
    w_full = lax.all_gather(w_qkv, "gz", axis=1, tiled=True)
    wo_full = lax.all_gather(w_out, "gz", axis=1, tiled=True)
    rows_block = w_full
    projected = jnp.einsum(
        "tc,mch->mth",
        lax.all_gather(normed, ("gx", "gy"), axis=1, tiled=True),
        rows_block,
        preferred_element_type=jnp.float32,
    )
    projected = projected.astype(jnp.bfloat16)
    queries = projected[0]
    keys_values = lax.all_gather(
        jnp.concatenate([projected[1], projected[2]], axis=1), "gz", axis=0, tiled=True
    )
    key_total = keys_values.shape[0]
    query_pos = lax.axis_index("gz") * tok_rows + jnp.arange(tok_rows, dtype=jnp.int32)
    query_span = span_index(query_pos, image_spans)
    key_block = 512
    block_count = key_total // key_block
    score_scale = 1.0 / math.sqrt(head_dim)
    block_ids = jnp.arange(block_count, dtype=jnp.int32)

    def block_scores(block_idx):
        first_key = block_idx * key_block
        kv_block = lax.dynamic_slice_in_dim(keys_values, first_key, key_block, 0)
        key_pos = first_key + jnp.arange(key_block, dtype=jnp.int32)
        allowed = visible(query_pos, query_span, key_pos, span_index(key_pos, image_spans))
        scores = (
            lax.dot_general(
                queries,
                kv_block[:, :head_dim],
                (((1,), (1,)), ((), ())),
                preferred_element_type=jnp.float32,
            )
            * score_scale
        )
        return (kv_block, allowed, scores)

    def gather_stats(state, block_idx):
        maxima, summed = state
        kv_block, allowed, scores = block_scores(block_idx)
        new_maxima = jnp.maximum(maxima, jnp.max(jnp.where(allowed, scores, masked_low), axis=1))
        fresh = jnp.sum(jnp.where(allowed, jnp.exp(scores - new_maxima[:, None]), 0.0), axis=1)
        return ((new_maxima, summed * jnp.exp(maxima - new_maxima) + fresh), None)

    start_state = (
        jnp.full((tok_rows,), masked_low, jnp.float32),
        jnp.zeros((tok_rows,), jnp.float32),
    )
    (maxima, summed), unused = lax.scan(gather_stats, start_state, block_ids)
    lse = maxima + jnp.log(summed)

    def block_probs(block_idx):
        kv_block, allowed, scores = block_scores(block_idx)
        return (kv_block, jnp.where(allowed, jnp.exp(scores - lse[:, None]), 0.0))

    def attend(accum, block_idx):
        kv_block, attn_p = block_probs(block_idx)
        return (
            accum
            + jnp.dot(
                attn_p.astype(jnp.bfloat16),
                kv_block[:, head_dim:],
                preferred_element_type=jnp.float32,
            ),
            None,
        )

    attended_f, unused = lax.scan(attend, jnp.zeros((tok_rows, head_dim), jnp.float32), block_ids)
    attended = attended_f.astype(jnp.bfloat16)
    all_heads = lax.all_gather(attended, ("gx", "gy"), axis=1, tiled=True)
    out_rows = lax.all_to_all(wo_full, ("gx", "gy"), split_axis=1, concat_axis=0, tiled=True)
    head_total = out_rows.shape[0] // head_dim
    per_head = jnp.einsum(
        "thd,hdc->htc",
        all_heads.reshape(tok_rows, head_total, head_dim),
        out_rows.reshape(head_total, head_dim, local_width),
        preferred_element_type=jnp.float32,
    )
    per_head = lax.optimization_barrier(per_head.astype(jnp.bfloat16)).astype(jnp.float32)
    attn_out = jnp.sum(per_head, axis=0).astype(jnp.bfloat16)
    segment = lax.all_gather(grad_out, ("gx", "gy"), axis=1, tiled=True)
    d_accum = lax.dot_general(
        segment, wo_full, (((1,), (1,)), ((), ())), preferred_element_type=jnp.float32
    )
    partial_value = lax.dot_general(
        attended, segment, (((0,), (0,)), ((), ())), preferred_element_type=jnp.float32
    )
    d_attended = d_accum.astype(jnp.bfloat16)
    row_dots = jnp.sum(d_attended.astype(jnp.float32) * attended.astype(jnp.float32), axis=1)

    def backward_block(d_query, block_idx):
        kv_block, attn_p = block_probs(block_idx)
        d_probs = lax.dot_general(
            d_attended,
            kv_block[:, head_dim:],
            (((1,), (1,)), ((), ())),
            preferred_element_type=jnp.float32,
        )
        d_scores = (attn_p * (d_probs - row_dots[:, None]) * score_scale).astype(jnp.bfloat16)
        d_query = d_query + jnp.dot(
            d_scores, kv_block[:, :head_dim], preferred_element_type=jnp.float32
        )
        d_keys = lax.dot_general(
            d_scores, queries, (((0,), (0,)), ((), ())), preferred_element_type=jnp.float32
        )
        d_values = lax.dot_general(
            attn_p.astype(jnp.bfloat16),
            d_attended,
            (((0,), (0,)), ((), ())),
            preferred_element_type=jnp.float32,
        )
        return (d_query, jnp.concatenate([d_keys, d_values], axis=1))

    d_query_f, kv_parts = lax.scan(
        backward_block, jnp.zeros((tok_rows, head_dim), jnp.float32), block_ids
    )
    kv_grad = lax.psum_scatter(
        kv_parts.reshape(key_total, 2 * head_dim).astype(jnp.bfloat16),
        "gz",
        scatter_dimension=0,
        tiled=True,
    ).astype(jnp.float32)
    grads = jnp.stack(
        [
            d_query_f.astype(jnp.bfloat16),
            kv_grad[:, :head_dim].astype(jnp.bfloat16),
            kv_grad[:, head_dim:].astype(jnp.bfloat16),
        ]
    )
    w_grad = jnp.einsum(
        "tc,mth->mch",
        lax.all_gather(normed, ("gx", "gy"), axis=1, tiled=True),
        grads,
        preferred_element_type=jnp.float32,
    )
    grad_qkv, grad_wout = (
        lax.psum_scatter(w_grad.astype(jnp.bfloat16), "gz", scatter_dimension=1, tiled=True).astype(
            jnp.float32
        ),
        lax.psum_scatter(
            partial_value.astype(jnp.bfloat16), "gz", scatter_dimension=1, tiled=True
        ).astype(jnp.float32),
    )
    rows_block = w_full
    grad_normed = (
        lax.psum_scatter(
            jnp.einsum("mch,mth->ct", rows_block, grads, preferred_element_type=jnp.float32).astype(
                jnp.bfloat16
            ),
            ("gx", "gy"),
            scatter_dimension=0,
            tiled=True,
        )
        .astype(jnp.float32)
        .T
    )
    upstream = grad_normed * row_gain
    norm_dots = lax.psum(jnp.sum(upstream * scaled, axis=1), ("gx", "gy"))
    grad_in = (inv_rms[:, None] * (upstream - scaled * (norm_dots / full_width)[:, None])).astype(
        jnp.bfloat16
    )
    onehot = (modality[:, None] == jnp.arange(2, dtype=jnp.int32)[None, :]).astype(jnp.float32)
    local_gain = jnp.dot(onehot.T, grad_normed * scaled, precision=lax.Precision.HIGHEST)
    grad_gain = lax.psum(local_gain, "gz")
    return (attn_out, grad_in, grad_qkv, grad_wout, grad_gain)


def solution(mesh):
    in_specs = (
        P("gz", ("gx", "gy")),
        P("gz"),
        P(),
        P(None, ("gx", "gy")),
        P(None, "gz", ("gx", "gy")),
        P(("gx", "gy"), "gz"),
        P("gz", ("gx", "gy")),
    )
    out_specs = (
        P("gz", ("gx", "gy")),
        P("gz", ("gx", "gy")),
        P(None, "gz", ("gx", "gy")),
        P(("gx", "gy"), "gz"),
        P(None, ("gx", "gy")),
    )
    return jax.shard_map(
        per_device, mesh=mesh, in_specs=in_specs, out_specs=out_specs, check_vma=False
    )
```

profile of v0, /device:TPU:0, one launch (start us, length us, event | category | flops | bytes accessed | tf_op | source)
XLA Modules:
  0.0 420.7 jit_solution(4267195177550142330)
XLA Ops:
  7.3 2.7 copy.44
  10.0 0.1 fusion.65
  10.2 35.2 %psum.21 = f32[512]{0:T(512)S(1)} all-reduce(f32[512]{0:T(512)S(1)} %fusion.65), channel_id=1, replica_groups=mesh['gx'=4,'gy'=4,'gz'=2] {'gx','gy'}, use_global_device_ids=true, to_apply=%region_1.0 | all-reduce | flops 512 | bytes 4096 | tf_op jit(solution)/shard_map/psum | solution.py:30
  45.4 0.9 fusion.66
  46.4 1.0 copy.50
  47.5 0.5 all-gather.14.cloned.1.call-update
  48.3 9.5 %all-gather.8.cloned.1.call-done = bf16[3,4096,128]{1,2,0:T(8,128)(2,1)} async-done(((bf16[3,2048,128]{1,2,0:T(8,128)(2,1)}), bf16[3,4096,128]{1,2,0:T(8,128)(2,1)}) %all-gather.8.cloned.1.call-update) | async-done | bytes 3145744 | tf_op jit(solution)/shard_map/all_gather | solution.py:35
  57.8 55.2 %all-gather.6.cloned.1.call-done = bf16[512,4096]{1,0:T(8,128)(2,1)} async-done(((bf16[512,256]{1,0:T(8,128)(2,1)}), bf16[512,4096]{1,0:T(8,128)(2,1)}) %all-gather.6.cloned.1.call-update) | async-done | bytes 4194320 | tf_op jit(solution)/shard_map/all_gather | solution.py:40
  113.0 5.0 %fusion.75 = f32[512,384]{0,1:S(1)} fusion(bf16[512,4096]{1,0:T(8,128)(2,1)} %all-gather.6.cloned.1.call-done, bf16[4096,384]{0,1:T(8,128)(2,1)} %bitcast.156), kind=kOutput, calls=%fused_computation.134 | convolution fusion | flops 1610612736 | bytes 8126464
  118.1 13.9 %all_gather.21 = bf16[1024,256]{0,1:T(8,128)(2,1)S(1)} all-gather(bf16[512,256]{0,1:T(8,128)(2,1)S(1)} %pad_maximum_fusion.1), channel_id=1, replica_groups=mesh['gx'=4,'gy'=4,'gz'=2] {'gz'}, dimensions={0}, use_global_device_ids=true | all-gather | bytes 786432 | tf_op jit(solution)/shard_map/all_gather | solution.py:46
  132.0 0.2 copy.47
  132.4 4.8 %while.43 = (s32[]{:T(128)}, f32[512]{0:T(512)S(1)}, f32[512]{0:T(512)S(1)}, s32[2]{0:T(128)S(1)}, s32[512]{0:T(512)S(1)}, /*index=5*/s32[2,8]{1,0:T(2,128)S(1)}...) while((s32[]{:T(128)}, f32[512]{0:T(512)S(1)}, ...), condition=%wide.region_7.8_spmd.clone, body=%wide.region_3.7_spmd.clone.sunk | while | flops 70803472 | bytes 2418638 | solution.py:84
  132.4 0.6 dynamic_slice.46
  133.7 0.5 select_reduce_fusion.12
  134.2 0.5 select_reduce_fusion.13
  134.8 0.6 dynamic_slice.46
  136.1 0.5 select_reduce_fusion.12
  136.6 0.5 select_reduce_fusion.13
  137.2 0.6 log_add_fusion
  137.7 5.9 %while.44 = (s32[]{:T(128)}, f32[512,128]{1,0:T(8,128)S(1)}, s32[2]{0:T(128)S(1)}, s32[512]{0:T(512)S(1)}, s32[2,8]{1,0:T(2,128)S(1)}, /*index=5*/bf16[1024,256]...) while((s32[]{:T(128)}, f32[512,128]{1,0:T(8,128)S(1)}, ...), condition=%wide.region_10.11_spmd.clone, body=%wide.region_8.10_spmd.clone.sunk | while | flops 136467984 | bytes 945628 | solution.py:103
  137.7 0.6 dynamic_slice.47
  139.1 1.5 fusion.118
  140.7 0.6 dynamic_slice.47
  142.1 1.5 fusion.118
  143.8 47.6 %all-gather.14.cloned.1.call-done = bf16[512,4096]{1,0:T(8,128)(2,1)} async-done(((bf16[512,256]{1,0:T(8,128)(2,1)}), bf16[512,4096]{1,0:T(8,128)(2,1)}) %all-gather.14.cloned.1.call-update) | async-done | bytes 4194320 | tf_op jit(solution)/shard_map/all_gather | solution.py:116
  191.3 4.0 multiply_reduce_fusion
  195.5 0.5 iota.88
  196.0 9.3 %while.45 = (s32[]{:T(128)}, f32[512,128]{1,0:T(8,128)S(1)}, bf16[2,512,256]{1,2,0:T(8,128)(2,1)S(1)}, s32[2]{0:T(128)}, s32[512]{0:T(512)S(1)}, /*index=5*/s32[...) while((s32[]{:T(128)}, f32[512,128]{1,0:T(8,128)S(1)}, ...), condition=%wide.region_15.16_spmd.clone, body=%wide.region_13.15_spmd.clone.sunk | while | flops 339367424 | bytes 6974985 | solution.py:149
  196.0 1.2 dynamic_slice.48
  198.0 1.2 fusion.129
  199.3 0.3 fusion.130
  199.6 0.3 fusion.132
  199.9 0.3 fusion.131
  200.2 0.4 convolution_add_fusion.2
  200.6 1.2 dynamic_slice.48
  202.7 1.2 fusion.129
  203.9 0.3 fusion.130
  204.2 0.3 fusion.132
  204.5 0.3 fusion.131
  204.9 0.4 convolution_add_fusion.2
  205.3 1.0 copy.56
  206.4 3.9 convolution_convert_fusion.1
  210.3 0.7 all-gather.10.cloned.1.call-update
  211.1 8.2 %reduce-scatter.5.cloned.1.call-done = bf16[512,256]{1,0:T(8,128)(2,1)} async-done(((bf16[1024,256]{1,0:T(8,128)(2,1)}), bf16[512,256]{1,0:T(8,128)(2,1)}) %reduce-scatter.5.cloned.1.call-update) | async-done | bytes 262160 | tf_op jit(solution)/shard_map/reduce_scatter | solution.py:152
  219.2 1.0 slice_bitcast_fusion.7
  220.2 5.8 %fusion.52 = bf16[4096,512]{0,1:T(8,128)(2,1)} fusion(bf16[3,4096,128]{1,2,0:T(8,128)(2,1)} %all-gather.8.cloned.1.call-done, bf16[1,512,128]{2,1,0:T(8,128)(2,1)S(1)} %get-tuple-element.678, bf16[1,512,128]{2,1,0:T(8,128)(2,1)S(1)} %get-tuple-element.677, bf16[1,512,128]{2,1,0:T(8,128)(2,1)S(1)} %convert_bitcast_fusion.1), kind=kOutput, calls=%fused_computation.84 | convolution fusion | flops 1613103104 | bytes 7733248 | tf_op jit(solution)/shard_map/mch,mth->ct/dot_general | solution.py:182
  226.1 0.2 reduce-scatter.9.cloned.1.call-start
  226.3 6.1 %fusion.53 = bf16[3,4096,128]{1,2,0:T(8,128)(2,1)} fusion(bf16[512,4096]{1,0:T(8,128)(2,1)} %all-gather.6.cloned.1.call-done, bf16[1,512,128]{2,1,0:T(8,128)(2,1)S(1)} %get-tuple-element.678, bf16[1,512,128]{2,1,0:T(8,128)(2,1)S(1)} %get-tuple-element.677, bf16[1,512,128]{2,1,0:T(8,128)(2,1)S(1)} %convert_bitcast_fusion.1), kind=kOutput, calls=%fused_computation.85 | convolution fusion | flops 1612578816 | bytes 7733248 | tf_op jit(solution)/shard_map/tc,mth->mch/dot_general | solution.py:165
  232.4 1.3 copy.51
  233.8 5.5 %all-to-all-start = ((bf16[128,16,256]{2,0,1:T(8,128)(2,1)}), bf16[128,16,256]{2,0,1:T(8,128)(2,1)S(1)}, u32[]{:S(2)}, u32[]{:S(2)}) async-start(bf16[128,16,256]{2,0,1:T(8,128)(2,1)} %copy.51), calls=%async_computation | async-start | bytes 2097152 | tf_op jit(solution)/shard_map/all_to_all | solution.py:106
  239.3 3.1 reduce-scatter.11.cloned.1.call-done
  242.4 2.1 convert_element_type.104
  244.5 25.8 %all-to-all-done = bf16[128,16,256]{2,0,1:T(8,128)(2,1)S(1)} async-done(((bf16[128,16,256]{2,0,1:T(8,128)(2,1)}), bf16[128,16,256]{2,0,1:T(8,128)(2,1)S(1)}, u32[]{:S(2)}, u32[]{:S(2)}) %all-to-all-start) | async-done | bytes 1048608 | tf_op jit(solution)/shard_map/all_to_all | solution.py:106
  270.3 19.1 %all-gather.10.cloned.1.call-done = bf16[512,2048]{0,1:T(8,128)(2,1)} async-done(((bf16[512,128]{0,1:T(8,128)(2,1)}), bf16[512,2048]{0,1:T(8,128)(2,1)}) %all-gather.10.cloned.1.call-update) | async-done | bytes 2097168 | tf_op jit(solution)/shard_map/all_gather | solution.py:105
  289.4 4.8 %convolution_convert_fusion.2 = bf16[16,512,256]{2,1,0:T(8,128)(2,1)} fusion(bf16[512,16,128]{0,2,1:T(8,128)(2,1)} %bitcast.147, bf16[128,16,256]{2,0,1:T(8,128)(2,1)S(1)} %all-to-all-done), kind=kOutput, calls=%fused_computation.88 | convolution fusion | flops 538968064 | bytes 7340032 | tf_op jit(solution)/shard_map/thd,hdc->htc/dot_general | solution.py:108
  294.2 3.5 reduce_sum.98
  297.8 67.0 %reduce-scatter.7.cloned.1.call-done = bf16[256,512]{0,1:T(8,128)(2,1)} async-done(((bf16[4096,512]{0,1:T(8,128)(2,1)}), bf16[256,512]{0,1:T(8,128)(2,1)}) %reduce-scatter.7.cloned.1.call-update) | async-done | bytes 262160 | tf_op jit(solution)/shard_map/reduce_scatter | solution.py:181
  364.8 1.3 fusion.59
  366.1 30.5 %psum.22 = f32[512]{0:T(512)S(1)} all-reduce(f32[512]{0:T(512)S(1)} %fusion.59), channel_id=1, replica_groups=mesh['gx'=4,'gy'=4,'gz'=2] {'gx','gy'}, use_global_device_ids=true, to_apply=%region_19.20 | all-reduce | flops 512 | bytes 4096 | tf_op jit(solution)/shard_map/psum | solution.py:193
  396.6 1.5 fusion.63
  398.1 5.7 %psum.23 = f32[2,256]{1,0:T(2,128)} all-reduce(f32[2,256]{1,0:T(2,128)S(1)} %fusion.63), channel_id=1, replica_groups=mesh['gx'=4,'gy'=4,'gz'=2] {'gz'}, use_global_device_ids=true, to_apply=%region_22.23 | all-reduce | flops 512 | bytes 4096 | tf_op jit(solution)/shard_map/psum | solution.py:199
  403.8 6.4 %reduce-scatter.9.cloned.1.call-done = bf16[3,2048,128]{1,2,0:T(8,128)(2,1)} async-done(((bf16[3,4096,128]{1,2,0:T(8,128)(2,1)}), bf16[3,2048,128]{1,2,0:T(8,128)(2,1)}) %reduce-scatter.9.cloned.1.call-update) | async-done | bytes 1572880 | tf_op jit(solution)/shard_map/reduce_scatter | solution.py:172
  410.2 3.1 copy.59
  413.2 1.0 fusion.62
  (113 shorter events, 1.9 us)
Async XLA Ops:
  7.2 2.8 copy-start
  7.2 38.2 %copy-start.12 = (s32[512]{0:T(512)S(1)}, s32[512]{0:T(512)}, u32[]{:S(2)}) copy-start(s32[512]{0:T(512)} %param.14) | copy-start | bytes 6148
  7.2 38.2 %copy-start.14 = (f32[2,256]{1,0:T(2,128)S(1)}, f32[2,256]{1,0:T(2,128)}, u32[]{:S(2)}) copy-start(f32[2,256]{1,0:T(2,128)} %param.16) | copy-start | bytes 6148
  7.2 39.2 %copy-start.4 = (bf16[128,2048]{1,0:T(8,128)(2,1)S(1)}, bf16[128,2048]{1,0:T(8,128)(2,1)}, u32[]{:S(2)}) copy-start(bf16[128,2048]{1,0:T(8,128)(2,1)} %param.18) | copy-start | bytes 1572868
  7.2 41.0 %copy-start.5 = (s32[2,8]{1,0:T(2,128)S(1)}, s32[2,8]{1,0:T(2,128)}, u32[]{:S(2)}) copy-start(s32[2,8]{1,0:T(2,128)} %param.15) | copy-start | bytes 196
  7.2 50.6 %all-gather.8.cloned.1.call-start = ((), (), s32[]{:S(2)}) async-start(), calls=%async_computation.6 | async-start | bytes 4718592 | tf_op jit(solution)/shard_map/all_gather | solution.py:35
  10.0 103.0 %all-gather.6.cloned.1.call-start = ((), (), s32[]{:S(2)}) async-start(), calls=%async_computation.5 | async-start | bytes 4456448 | tf_op jit(solution)/shard_map/all_gather | solution.py:40
  45.4 2.8 copy-start.10
  45.4 2.7 copy-start.8
  45.4 72.6 %copy-start.6 = (f32[1,256]{1,0:T(1,128)}, f32[1,256]{1,0:T(1,128)S(1)}, u32[]{:S(2)}) copy-start(f32[1,256]{1,0:T(1,128)S(1)} %get-tuple-element.679) | copy-start | bytes 3076
  46.3 97.4 %all-gather.12.cloned.1.call-start = ((), (), s32[]{:S(2)}) async-start(), calls=%async_computation.8 | async-start | bytes 1572864 | tf_op jit(solution)/shard_map/all_gather | solution.py:36
  47.4 143.9 %all-gather.14.cloned.1.call-start = ((), (), s32[]{:S(2)}) async-start(), calls=%async_computation.9 | async-start | bytes 4456448 | tf_op jit(solution)/shard_map/all_gather | solution.py:116
  48.0 171.2 %reduce-scatter.5.cloned.1.call-start = ((), (), s32[]{:S(2)}) async-start(), calls=%async_computation.10 | async-start | bytes 786432 | tf_op jit(solution)/shard_map/reduce_scatter | solution.py:152
  143.7 62.6 %copy-start.2 = (bf16[512,128]{0,1:T(8,128)(2,1)}, bf16[512,128]{0,1:T(8,128)(2,1)S(1)}, u32[]{:S(2)}) copy-start(bf16[512,128]{0,1:T(8,128)(2,1)S(1)} %copy.49) | copy-start | bytes 393220
  206.3 36.1 %reduce-scatter.11.cloned.1.call-start = ((), (), s32[]{:S(2)}) async-start(), calls=%async_computation.13 | async-start | bytes 1572864 | tf_op jit(solution)/shard_map/reduce_scatter | solution.py:175
  210.3 79.1 %all-gather.10.cloned.1.call-start = ((), (), s32[]{:S(2)}) async-start(), calls=%async_computation.7 | async-start | bytes 2228224 | tf_op jit(solution)/shard_map/all_gather | solution.py:105
  211.0 153.8 %reduce-scatter.7.cloned.1.call-start = ((), (), s32[]{:S(2)}) async-start(), calls=%async_computation.11 | async-start | bytes 4456448 | tf_op jit(solution)/shard_map/reduce_scatter | solution.py:181
  226.1 6.4 %copy-start.1 = (bf16[128,4096]{0,1:T(8,128)(2,1)S(1)}, bf16[128,4096]{0,1:T(8,128)(2,1)}, u32[]{:S(2)}) copy-start(bf16[128,4096]{0,1:T(8,128)(2,1)} %all-gather.12.cloned.1.call-done) | copy-start | bytes 3145732
  226.1 184.1 %reduce-scatter.9.cloned.1.call-start = ((), (), s32[]{:S(2)}) async-start(), calls=%async_computation.12 | async-start | bytes 4718592 | tf_op jit(solution)/shard_map/reduce_scatter | solution.py:172
  233.8 36.5 %all-to-all-start = ((bf16[128,16,256]{2,0,1:T(8,128)(2,1)}), bf16[128,16,256]{2,0,1:T(8,128)(2,1)S(1)}, u32[]{:S(2)}, u32[]{:S(2)}) async-start(bf16[128,16,256]{2,0,1:T(8,128)(2,1)} %copy.51), calls=%async_computation | async-start | bytes 2097152 | tf_op jit(solution)/shard_map/all_to_all | solution.py:106
  289.4 75.4 %copy-start.7 = (f32[1,256]{1,0:T(1,128)S(1)}, f32[1,256]{1,0:T(1,128)}, u32[]{:S(2)}) copy-start(f32[1,256]{1,0:T(1,128)} %copy-done.6) | copy-start | bytes 3076
  289.4 75.4 %copy-start.9 = (f32[1,256]{1,0:T(1,128)S(1)}, f32[1,256]{1,0:T(1,128)}, u32[]{:S(2)}) copy-start(f32[1,256]{1,0:T(1,128)} %copy-done.8) | copy-start | bytes 3076
  289.4 75.4 %copy-start.11 = (pred[512]{0:T(512)(128)(4,1)S(1)}, pred[512]{0:T(512)(128)(4,1)}, u32[]{:S(2)}) copy-start(pred[512]{0:T(512)(128)(4,1)} %copy-done.10) | copy-start | bytes 1540
  294.2 102.4 %copy-start.13 = (s32[512]{0:T(512)S(1)}, s32[512]{0:T(512)}, u32[]{:S(2)}) copy-start(s32[512]{0:T(512)} %param.14) | copy-start | bytes 6148
  364.8 48.5 %copy-start.3 = (bf16[256,512]{0,1:T(8,128)(2,1)S(1)}, bf16[256,512]{0,1:T(8,128)(2,1)}, u32[]{:S(2)}) copy-start(bf16[256,512]{0,1:T(8,128)(2,1)} %reduce-scatter.7.cloned.1.call-done) | copy-start | bytes 786436
Sparse Core Ops, SparseCore 0:
  10.1 47.6 all-gather.7
  60.5 52.4 all-gather.5
  115.1 23.5 all-gather.11
  140.6 50.6 all-gather.13
  206.4 12.7 reduce-scatter.4
  221.9 20.3 reduce-scatter.10
  245.1 44.2 all-gather.9
  293.3 71.4 reduce-scatter.6
  367.6 42.5 reduce-scatter.8
where the time goes:
time: 421 us
  waiting for transfers between devices  243 us (58%)
  blocking collectives  85.3 us (20%)
  matrix products  40.2 us (10%)
  local copies, waits for them, and re-layouts  16.1 us (4%)
  between operations  14.2 us (3%)
  other arithmetic  11.5 us (3%)
  starting transfers between devices  6.02 us (1%)
  loops' own time  4.31 us (1%)
    reduce_scatter x1, waiting for transfers between devices, per_device(): lax.psum_scatter(jnp.einsum('mch,mth->ct', rows_block, grads, preferred_e...  67 us
    all_gather x1, waiting for transfers between devices, per_device(): lax.all_gather(normed, ('gx', 'gy'), axis=1, tiled=True)  55.2 us
    all_gather x1, waiting for transfers between devices, per_device(): segment = lax.all_gather(grad_out, ('gx', 'gy'), axis=1, tiled=True)  47.6 us
    psum x1, blocking collectives, per_device(): squares = lax.psum(jnp.sum(inputs_f * inputs_f, axis=1), ('gx', 'gy'))  35.2 us
    psum x1, blocking collectives, per_device(): norm_dots = lax.psum(jnp.sum(upstream * scaled, axis=1), ('gx', 'gy'))  30.5 us
    all_to_all x1, waiting for transfers between devices, per_device(): lax.all_to_all(wo_full, ('gx', 'gy'), split_axis=1, concat_axis=0, tiled=...  25.8 us
    all_gather x1, waiting for transfers between devices, per_device(): all_heads = lax.all_gather(attended, ('gx', 'gy'), axis=1, tiled=True)  19.1 us
    all_gather x1, blocking collectives, per_device(): lax.all_gather(jnp.concatenate([projected[1], projected[2]], axis=1), 'gz...  13.9 us
  transfers between devices with their start and end apart: 10, of which 9 were waited for; matrix products, arithmetic and copies ran while one was open for 11% of the time, Pallas kernels for 0%

commit v1 on v0

--- a/solution.py
+++ b/solution.py
@@ -113,7 +113,13 @@
     )
     per_head = lax.optimization_barrier(per_head.astype(jnp.bfloat16)).astype(jnp.float32)
     attn_out = jnp.sum(per_head, axis=0).astype(jnp.bfloat16)
-    segment = lax.all_gather(grad_out, ("gx", "gy"), axis=1, tiled=True)
+
+    def _load_waves(work_x, ax_name):
+        current_value = jax.lax.all_gather(work_x, axis_name=ax_name)
+        v_now = jnp.concatenate(current_value, axis=1)
+        return v_now
+
+    segment = _load_waves(grad_out, ("gx", "gy"))
     d_accum = lax.dot_general(
         segment, wo_full, (((1,), (1,)), ((), ())), preferred_element_type=jnp.float32
     )

time: 421 us -> 413 us (0.981)
  waiting for transfers between devices: 243 us -> 237 us
  blocking collectives: 85.3 us -> 80.5 us
  local copies, waits for them, and re-layouts: 16.1 us -> 20.7 us
    all_gather x1, waiting for transfers between devices: 47.6 us -> 26.9 us  [_load_waves(): current_value = jax.lax.all_gather(work_x, axis_name=ax_name)]
    all_gather x1, waiting for transfers between devices: 0.02 us -> 15.3 us  [per_device(): wo_full = lax.all_gather(w_out, 'gz', axis=1, tiled=True)]
    reshape x0 -> x1, local copies, waits for them, and re-layouts: none -> 6.43 us  [_load_waves(): v_now = jnp.concatenate(current_value, axis=1)]
    all_gather x1, blocking collectives: 13.9 us -> 9.12 us  [per_device(): lax.all_gather(jnp.concatenate([projected[1], projected[2]], axis=1), 'gz...]
  transfers between devices with their start and end apart: 10 -> 10, of which waited for: 9 -> 10; matrix products, arithmetic and copies ran while one was open for 11% -> 13% of each run, Pallas kernels for 0% -> 0%
where the time goes in v1:
time: 413 us; the launch traced here: 412 us
  waiting for transfers between devices  237 us (57%)
  blocking collectives  80.5 us (19%)
  matrix products  37.4 us (9%)
  local copies, waits for them, and re-layouts  20.7 us (5%)
  between operations  14.2 us (3%)
  other arithmetic  11.8 us (3%)
  starting transfers between devices  6.03 us (1%)
  loops' own time  4.36 us (1%)
    reduce_scatter x1, waiting for transfers between devices, per_device(): lax.psum_scatter(jnp.einsum('mch,mth->ct', rows_block, grads, preferred_e...  67 us
    all_gather x1, waiting for transfers between devices, per_device(): lax.all_gather(normed, ('gx', 'gy'), axis=1, tiled=True)  55.2 us
    psum x1, blocking collectives, per_device(): squares = lax.psum(jnp.sum(inputs_f * inputs_f, axis=1), ('gx', 'gy'))  35.2 us
    psum x1, blocking collectives, per_device(): norm_dots = lax.psum(jnp.sum(upstream * scaled, axis=1), ('gx', 'gy'))  30.5 us
    all_gather x1, waiting for transfers between devices, _load_waves(): current_value = jax.lax.all_gather(work_x, axis_name=ax_name)  26.9 us
    all_to_all x1, waiting for transfers between devices, per_device(): lax.all_to_all(wo_full, ('gx', 'gy'), split_axis=1, concat_axis=0, tiled=...  25.8 us
    all_gather x1, waiting for transfers between devices, per_device(): all_heads = lax.all_gather(attended, ('gx', 'gy'), axis=1, tiled=True)  19.1 us
    all_gather x1, waiting for transfers between devices, per_device(): wo_full = lax.all_gather(w_out, 'gz', axis=1, tiled=True)  15.3 us
  transfers between devices with their start and end apart: 10, of which 10 were waited for; matrix products, arithmetic and copies ran while one was open for 13% of the time, Pallas kernels for 0%

profile of v1, /device:TPU:0, one launch (start us, length us, event | category | flops | bytes accessed | tf_op | source)
XLA Modules:
  0.0 412.0 jit_solution(1653169652756862813)
XLA Ops:
  7.3 2.7 copy.62
  10.0 0.1 fusion.65
  10.2 35.2 %psum.21 = f32[512]{0:T(512)S(1)} all-reduce(f32[512]{0:T(512)S(1)} %fusion.65), channel_id=1, replica_groups=mesh['gx'=4,'gy'=4,'gz'=2] {'gx','gy'}, use_global_device_ids=true, to_apply=%region_1.0 | all-reduce | flops 512 | bytes 4096 | tf_op jit(solution)/shard_map/psum | solution.py:30
  45.4 0.9 fusion.66
  46.4 0.7 all-gather.15.cloned.1.call-update
  47.1 1.0 copy.68
  48.4 9.4 %all-gather.9.cloned.1.call-done = bf16[3,4096,128]{1,2,0:T(8,128)(2,1)} async-done(((bf16[3,2048,128]{1,2,0:T(8,128)(2,1)}), bf16[3,4096,128]{1,2,0:T(8,128)(2,1)}) %all-gather.9.cloned.1.call-update) | async-done | bytes 3145744 | tf_op jit(solution)/shard_map/all_gather | solution.py:35
  57.8 55.2 %all-gather.7.cloned.1.call-done = bf16[512,4096]{1,0:T(8,128)(2,1)} async-done(((bf16[512,256]{1,0:T(8,128)(2,1)}), bf16[512,4096]{1,0:T(8,128)(2,1)}) %all-gather.7.cloned.1.call-update) | async-done | bytes 4194320 | tf_op jit(solution)/shard_map/all_gather | solution.py:40
  113.0 5.0 %fusion.75 = f32[512,384]{0,1:S(1)} fusion(bf16[512,4096]{1,0:T(8,128)(2,1)} %all-gather.7.cloned.1.call-done, bf16[4096,384]{0,1:T(8,128)(2,1)} %bitcast.163), kind=kOutput, calls=%fused_computation.134 | convolution fusion | flops 1610612736 | bytes 8126464
  118.2 9.1 %all_gather.24 = bf16[1024,256]{0,1:T(8,128)(2,1)S(1)} all-gather(bf16[512,256]{0,1:T(8,128)(2,1)S(1)} %pad_maximum_fusion.1), channel_id=1, replica_groups=mesh['gx'=4,'gy'=4,'gz'=2] {'gz'}, dimensions={0}, use_global_device_ids=true | all-gather | bytes 786432 | tf_op jit(solution)/shard_map/all_gather | solution.py:46
  127.3 0.2 copy.65
  127.5 4.8 %while.43 = (s32[]{:T(128)}, f32[512]{0:T(512)S(1)}, f32[512]{0:T(512)S(1)}, s32[2]{0:T(128)S(1)}, s32[512]{0:T(512)S(1)}, /*index=5*/s32[2,8]{1,0:T(2,128)S(1)}...) while((s32[]{:T(128)}, f32[512]{0:T(512)S(1)}, ...), condition=%wide.region_7.8_spmd.clone, body=%wide.region_3.7_spmd.clone.sunk | while | flops 70803472 | bytes 2418646 | solution.py:84
  127.6 0.6 dynamic_slice.46
  128.9 0.5 select_reduce_fusion.12
  129.4 0.5 select_reduce_fusion.13
  130.0 0.6 dynamic_slice.46
  131.3 0.5 select_reduce_fusion.12
  131.8 0.5 select_reduce_fusion.13
  132.4 4.5 %while.44 = (s32[]{:T(128)}, f32[512,128]{1,0:T(8,128)S(1)}, s32[2]{0:T(128)S(1)}, s32[512]{0:T(512)S(1)}, s32[2,8]{1,0:T(2,128)S(1)}, /*index=5*/bf16[1024,256]...) while((s32[]{:T(128)}, f32[512,128]{1,0:T(8,128)S(1)}, ...), condition=%wide.region_10.11_spmd.clone, body=%wide.region_8.10_spmd.clone.sunk | while | flops 136467984 | bytes 945636 | solution.py:103
  132.4 0.6 dynamic_slice.47
  133.8 0.9 fusion.118
  134.7 0.6 dynamic_slice.47
  136.0 0.8 fusion.118
  136.9 26.9 %all-gather.15.cloned.1.call-done = bf16[8192,256]{1,0:T(8,128)(2,1)} async-done(((bf16[512,256]{1,0:T(8,128)(2,1)}), bf16[8192,256]{1,0:T(8,128)(2,1)}) %all-gather.15.cloned.1.call-update) | async-done | bytes 4194320 | tf_op jit(solution)/shard_map/all_gather | solution.py:118
  163.8 6.4 %copy.71 = bf16[512,16,256]{0,2,1:T(8,128)(2,1)} copy(bf16[512,16,256]{2,0,1:T(8,128)(2,1)} %bitcast.152) | data formatting | bytes 8388608 | tf_op jit(solution)/shard_map/reshape | solution.py:119
  170.4 15.3 %all-gather.13.cloned.1.call-done = bf16[128,4096]{0,1:T(8,128)(2,1)} async-done(((bf16[128,2048]{0,1:T(8,128)(2,1)}), bf16[128,4096]{0,1:T(8,128)(2,1)}) %all-gather.13.cloned.1.call-update) | async-done | bytes 1048592 | tf_op jit(solution)/shard_map/all_gather | solution.py:36
  185.6 3.3 multiply_reduce_fusion
  189.1 6.6 %while.45 = (s32[]{:T(128)}, f32[512,128]{1,0:T(8,128)S(1)}, bf16[2,512,256]{1,2,0:T(8,128)(2,1)S(1)}, s32[2]{0:T(128)S(1)}, s32[512]{0:T(512)S(1)}, /*index=5*/...) while((s32[]{:T(128)}, f32[512,128]{1,0:T(8,128)S(1)}, ...), condition=%wide.region_15.16_spmd.clone, body=%wide.region_13.15_spmd.clone.sunk | while | flops 339367424 | bytes 6974993 | solution.py:155
  189.1 0.6 dynamic_slice.48
  190.5 0.5 fusion.129
  191.0 0.3 fusion.131
  191.3 0.3 fusion.130
  191.6 0.3 fusion.132
  192.0 0.4 convolution_add_fusion.2
  192.4 0.6 dynamic_slice.48
  193.8 0.5 fusion.129
  194.3 0.3 fusion.131
  194.7 0.3 fusion.130
  195.0 0.3 fusion.132
  195.3 0.4 convolution_add_fusion.2
  195.7 1.0 copy.75
  196.8 4.6 %convolution_convert_fusion.1 = bf16[128,4096]{1,0:T(8,128)(2,1)} fusion(bf16[512,128]{0,1:T(8,128)(2,1)S(1)} %copy.67, bf16[512,4096]{0,1:T(8,128)(2,1)} %bitcast.151), kind=kOutput, calls=%fused_computation.86 | convolution fusion | flops 537395200 | bytes 5373952 | tf_op jit(solution)/shard_map/dot_general | solution.py:126
  201.5 0.7 all-gather.11.cloned.1.call-update
  202.3 9.2 %reduce-scatter.5.cloned.1.call-done = bf16[512,256]{1,0:T(8,128)(2,1)} async-done(((bf16[1024,256]{1,0:T(8,128)(2,1)}), bf16[512,256]{1,0:T(8,128)(2,1)}) %reduce-scatter.5.cloned.1.call-update) | async-done | bytes 262160 | tf_op jit(solution)/shard_map/reduce_scatter | solution.py:158
  211.5 1.0 slice_bitcast_fusion.7
  212.5 5.8 %fusion.52 = bf16[4096,512]{0,1:T(8,128)(2,1)} fusion(bf16[3,4096,128]{1,2,0:T(8,128)(2,1)} %all-gather.9.cloned.1.call-done, bf16[1,512,128]{2,1,0:T(8,128)(2,1)S(1)} %get-tuple-element.713, bf16[1,512,128]{2,1,0:T(8,128)(2,1)S(1)} %get-tuple-element.712, bf16[1,512,128]{2,1,0:T(8,128)(2,1)S(1)} %convert_bitcast_fusion.1), kind=kOutput, calls=%fused_computation.84 | convolution fusion | flops 1613103104 | bytes 7733248 | tf_op jit(solution)/shard_map/mch,mth->ct/dot_general | solution.py:188
  218.3 0.2 reduce-scatter.9.cloned.1.call-start
  218.5 6.1 %fusion.53 = bf16[3,4096,128]{1,2,0:T(8,128)(2,1)} fusion(bf16[512,4096]{1,0:T(8,128)(2,1)} %all-gather.7.cloned.1.call-done, bf16[1,512,128]{2,1,0:T(8,128)(2,1)S(1)} %get-tuple-element.713, bf16[1,512,128]{2,1,0:T(8,128)(2,1)S(1)} %get-tuple-element.712, bf16[1,512,128]{2,1,0:T(8,128)(2,1)S(1)} %convert_bitcast_fusion.1), kind=kOutput, calls=%fused_computation.85 | convolution fusion | flops 1612578816 | bytes 7733248 | tf_op jit(solution)/shard_map/tc,mth->mch/dot_general | solution.py:171
  224.7 1.3 copy.69
  226.0 5.5 %all-to-all-start = ((bf16[128,16,256]{2,0,1:T(8,128)(2,1)}), bf16[128,16,256]{2,0,1:T(8,128)(2,1)S(1)}, u32[]{:S(2)}, u32[]{:S(2)}) async-start(bf16[128,16,256]{2,0,1:T(8,128)(2,1)} %copy.69), calls=%async_computation | async-start | bytes 2097152 | tf_op jit(solution)/shard_map/all_to_all | solution.py:106
  231.5 3.1 reduce-scatter.11.cloned.1.call-done
  234.6 2.1 convert_element_type.104
  236.7 25.8 %all-to-all-done = bf16[128,16,256]{2,0,1:T(8,128)(2,1)S(1)} async-done(((bf16[128,16,256]{2,0,1:T(8,128)(2,1)}), bf16[128,16,256]{2,0,1:T(8,128)(2,1)S(1)}, u32[]{:S(2)}, u32[]{:S(2)}) %all-to-all-start) | async-done | bytes 1048608 | tf_op jit(solution)/shard_map/all_to_all | solution.py:106
  262.5 19.1 %all-gather.11.cloned.1.call-done = bf16[512,2048]{0,1:T(8,128)(2,1)} async-done(((bf16[512,128]{0,1:T(8,128)(2,1)}), bf16[512,2048]{0,1:T(8,128)(2,1)}) %all-gather.11.cloned.1.call-update) | async-done | bytes 2097168 | tf_op jit(solution)/shard_map/all_gather | solution.py:105
  281.6 4.8 %convolution_convert_fusion.2 = bf16[16,512,256]{2,1,0:T(8,128)(2,1)} fusion(bf16[512,16,128]{0,2,1:T(8,128)(2,1)} %bitcast.153, bf16[128,16,256]{2,0,1:T(8,128)(2,1)S(1)} %all-to-all-done), kind=kOutput, calls=%fused_computation.88 | convolution fusion | flops 538968064 | bytes 7340032 | tf_op jit(solution)/shard_map/thd,hdc->htc/dot_general | solution.py:108
  286.4 3.5 reduce_sum.98
  290.0 67.0 %reduce-scatter.7.cloned.1.call-done = bf16[256,512]{0,1:T(8,128)(2,1)} async-done(((bf16[4096,512]{0,1:T(8,128)(2,1)}), bf16[256,512]{0,1:T(8,128)(2,1)}) %reduce-scatter.7.cloned.1.call-update) | async-done | bytes 262160 | tf_op jit(solution)/shard_map/reduce_scatter | solution.py:187
  357.0 1.2 fusion.59
  358.2 30.5 %psum.22 = f32[512]{0:T(512)S(1)} all-reduce(f32[512]{0:T(512)S(1)} %fusion.59), channel_id=1, replica_groups=mesh['gx'=4,'gy'=4,'gz'=2] {'gx','gy'}, use_global_device_ids=true, to_apply=%region_19.20 | all-reduce | flops 512 | bytes 4096 | tf_op jit(solution)/shard_map/psum | solution.py:199
  388.8 1.5 fusion.63
  390.2 5.7 %psum.23 = f32[2,256]{1,0:T(2,128)} all-reduce(f32[2,256]{1,0:T(2,128)S(1)} %fusion.63), channel_id=1, replica_groups=mesh['gx'=4,'gy'=4,'gz'=2] {'gz'}, use_global_device_ids=true, to_apply=%region_22.23 | all-reduce | flops 512 | bytes 4096 | tf_op jit(solution)/shard_map/psum | solution.py:205
  395.9 1.9 fusion.62
  397.9 4.5 %reduce-scatter.9.cloned.1.call-done = bf16[3,2048,128]{1,2,0:T(8,128)(2,1)} async-done(((bf16[3,4096,128]{1,2,0:T(8,128)(2,1)}), bf16[3,2048,128]{1,2,0:T(8,128)(2,1)}) %reduce-scatter.9.cloned.1.call-update) | async-done | bytes 1572880 | tf_op jit(solution)/shard_map/reduce_scatter | solution.py:178
  402.4 3.1 copy.78
  (98 shorter events, 1.8 us)
Async XLA Ops:
  7.2 2.8 copy-start
  7.2 38.2 %copy-start.5 = (s32[512]{0:T(512)S(1)}, s32[512]{0:T(512)}, u32[]{:S(2)}) copy-start(s32[512]{0:T(512)} %param.14) | copy-start | bytes 6148
  7.2 38.2 %copy-start.6 = (f32[2,256]{1,0:T(2,128)S(1)}, f32[2,256]{1,0:T(2,128)}, u32[]{:S(2)}) copy-start(f32[2,256]{1,0:T(2,128)} %param.16) | copy-start | bytes 6148
  7.2 39.9 %copy-start.3 = (bf16[128,2048]{1,0:T(8,128)(2,1)S(1)}, bf16[128,2048]{1,0:T(8,128)(2,1)}, u32[]{:S(2)}) copy-start(bf16[128,2048]{1,0:T(8,128)(2,1)} %param.18) | copy-start | bytes 1572868
  7.2 41.0 %copy-start.4 = (s32[2,8]{1,0:T(2,128)S(1)}, s32[2,8]{1,0:T(2,128)}, u32[]{:S(2)}) copy-start(s32[2,8]{1,0:T(2,128)} %param.15) | copy-start | bytes 196
  7.2 50.6 %all-gather.9.cloned.1.call-start = ((), (), s32[]{:S(2)}) async-start(), calls=%async_computation.6 | async-start | bytes 4718592 | tf_op jit(solution)/shard_map/all_gather | solution.py:35
  10.0 103.0 %all-gather.7.cloned.1.call-start = ((), (), s32[]{:S(2)}) async-start(), calls=%async_computation.5 | async-start | bytes 4456448 | tf_op jit(solution)/shard_map/all_gather | solution.py:40
  46.3 117.5 %all-gather.15.cloned.1.call-start = ((), (), s32[]{:S(2)}) async-start(), calls=%async_computation.13 | async-start | bytes 4456448 | tf_op jit(solution)/shard_map/all_gather | solution.py:118
  47.1 138.6 %all-gather.13.cloned.1.call-start = ((), (), s32[]{:S(2)}) async-start(), calls=%async_computation.8 | async-start | bytes 1572864 | tf_op jit(solution)/shard_map/all_gather | solution.py:36
  48.1 163.4 %reduce-scatter.5.cloned.1.call-start = ((), (), s32[]{:S(2)}) async-start(), calls=%async_computation.9 | async-start | bytes 786432 | tf_op jit(solution)/shard_map/reduce_scatter | solution.py:158
  170.3 26.4 %copy-start.1 = (bf16[512,128]{0,1:T(8,128)(2,1)}, bf16[512,128]{0,1:T(8,128)(2,1)S(1)}, u32[]{:S(2)}) copy-start(bf16[512,128]{0,1:T(8,128)(2,1)S(1)} %copy.67) | copy-start | bytes 393220
  196.7 37.9 %reduce-scatter.11.cloned.1.call-start = ((), (), s32[]{:S(2)}) async-start(), calls=%async_computation.12 | async-start | bytes 1572864 | tf_op jit(solution)/shard_map/reduce_scatter | solution.py:181
  201.4 80.2 %all-gather.11.cloned.1.call-start = ((), (), s32[]{:S(2)}) async-start(), calls=%async_computation.7 | async-start | bytes 2228224 | tf_op jit(solution)/shard_map/all_gather | solution.py:105
  202.2 154.8 %reduce-scatter.7.cloned.1.call-start = ((), (), s32[]{:S(2)}) async-start(), calls=%async_computation.10 | async-start | bytes 4456448 | tf_op jit(solution)/shard_map/reduce_scatter | solution.py:187
  218.3 6.4 %copy-start.2 = (bf16[128,4096]{0,1:T(8,128)(2,1)S(1)}, bf16[128,4096]{0,1:T(8,128)(2,1)}, u32[]{:S(2)}) copy-start(bf16[128,4096]{0,1:T(8,128)(2,1)} %all-gather.13.cloned.1.call-done) | copy-start | bytes 3145732
  218.3 184.1 %reduce-scatter.9.cloned.1.call-start = ((), (), s32[]{:S(2)}) async-start(), calls=%async_computation.11 | async-start | bytes 4718592 | tf_op jit(solution)/shard_map/reduce_scatter | solution.py:178
  226.0 36.5 %all-to-all-start = ((bf16[128,16,256]{2,0,1:T(8,128)(2,1)}), bf16[128,16,256]{2,0,1:T(8,128)(2,1)S(1)}, u32[]{:S(2)}, u32[]{:S(2)}) async-start(bf16[128,16,256]{2,0,1:T(8,128)(2,1)} %copy.69), calls=%async_computation | async-start | bytes 2097152 | tf_op jit(solution)/shard_map/all_to_all | solution.py:106
Sparse Core Ops, SparseCore 0:
  10.1 47.6 all-gather.8
  60.5 52.4 all-gather.6
  115.2 48.5 all-gather.14
  165.8 19.8 all-gather.12
  196.8 14.6 reduce-scatter.4
  214.2 20.3 reduce-scatter.10
  237.4 44.1 all-gather.10
  285.5 71.4 reduce-scatter.6
  359.8 42.5 reduce-scatter.8
